TPU v7x, 256 devices: a whole 4x4x8 slice. The times are simulated.
256 devices in a mesh: seq: 16 (over y, x), grp: 16 (over z, core).
Axes of the slice: x: 4, y: 4, z: 8, core: 2. Of those that a mesh axis runs over, the one named last changes fastest.
Arguments:
- actions: int32 [32, 7], P('grp'), may hold values from 0 to 255
- lengths: int32 [32], P('grp'), may hold values from 2048 to 4096
- embed: bfloat16 [256, 4096], replicated, may hold values from -6 to 6
- attn_gain: float32 [4096], replicated, may hold values from 0.1 to 1.9
- w_query: bfloat16 [4096, 4096], P('grp', 'seq'), may hold values from -0.09375 to 0.09375
- w_key: bfloat16 [4096, 4096], P('grp', 'seq'), may hold values from -0.140625 to 0.140625
- w_value: bfloat16 [4096, 4096], P('grp', 'seq'), may hold values from -0.09375 to 0.09375
- w_out: bfloat16 [4096, 4096], P('grp', 'seq'), may hold values from -0.09375 to 0.09375
- key_cache: bfloat16 [32, 4096, 4096], P('grp', 'seq'), may hold values from -136 to 136
- value_cache: bfloat16 [32, 4096, 4096], P('grp', 'seq'), may hold values from -6 to 6
- final_gain: float32 [4096], replicated, may hold values from 0.1 to 1.9
- head: bfloat16 [256, 4096], P('seq'), may hold values from -0.25 to 0.25
Outputs:
- logprob: float32 [32, 7, 256], P('grp', None, 'seq')
Inputs may be any that keep to these rules, and one draw needn't show every extreme that they name: Robot r's prompt occupies cache positions 0 to lengths[r] - 1.
All inputs are finite; a program needn't handle non-finite values.
Results may differ from a plain program's by a relative error of at most 0.008.
Values may be sent and summed in bfloat16 or wider, within the bound.
No kernel may reach another device: no remote copies, remote signals or barrier semaphores. Data moves between devices by JAX's collectives and lax.ppermute only.
A program may use at most 64 MiB of HBM per device.

v0:
```python
import jax
import jax.numpy as jnp
from jax import lax
from jax.sharding import Mesh
from jax.sharding import PartitionSpec as P

HEAD_DIM = 128
SEQ = ("seq_0", "seq_1")


def split_up(shard, dim, devices):
    before, after = (shard.shape[:dim], shard.shape[dim + 1 :])
    return jnp.moveaxis(shard.reshape(*before, devices, -1, *after), dim, 0)


def sum_at_owner(shard, axis, dim):
    pieces = split_up(shard, dim, lax.axis_size(axis))
    arrived = lax.all_to_all(pieces, axis, split_axis=0, concat_axis=0, tiled=True)
    return arrived.sum(axis=0)


def sent_together(arrays, axis, dim, along):
    widths = [a.shape[along] for a in arrays]
    both = jnp.concatenate(arrays, axis=along)
    out = lax.all_gather(both, axis, axis=dim, tiled=True)
    return tuple(jnp.split(out, [sum(widths[:k]) for k in range(1, len(widths))], axis=along))


def all_in_one(shard, axis):
    leaves = jax.tree.leaves(shard)
    order = sorted(range(len(leaves)), key=lambda k: -leaves[k].size)
    width = (1, *leaves[order[0]].shape)[-1]
    lines = [
        jnp.pad(leaves[k].reshape(-1), (0, -leaves[k].size % width)).reshape(-1, width)
        for k in order
    ]
    both, at, found = (lax.all_gather(jnp.concatenate(lines), axis), 0, {})
    for k, line in zip(order, lines):
        share = both[:, at : at + len(line)].reshape(len(both), -1)
        found[k] = share[:, : leaves[k].size].reshape(-1, *leaves[k].shape)
        at += len(line)
    numbers = iter(range(len(leaves)))
    return jax.tree.map(lambda _: found[next(numbers)], shard)


def merged_by_axis(shard, axes, combine):
    for axis in axes:
        pieces = all_in_one(shard, axis)
        shard = jax.tree.map(lambda part: part[0], pieces)
        for k in range(1, lax.axis_size(axis)):
            shard = combine(shard, jax.tree.map(lambda part: part[k], pieces))
    return shard


def sum_at_owner_2(shard, axis, dim):
    devices = lax.axis_size(axis)
    pieces = lax.all_to_all(split_up(shard, dim, devices), axis, 0, 0, tiled=True)
    return jnp.sum(pieces.astype(jnp.float32), axis=0)


def joined_along(pieces, dim):
    pieces = jnp.moveaxis(pieces, 0, dim)
    lengths = pieces.shape
    return pieces.reshape(*lengths[:dim], lengths[dim] * lengths[dim + 1], *lengths[dim + 2 :])


def copy_for_each(shard, axis):
    devices = lax.axis_size(axis)
    return lax.all_to_all(
        jnp.broadcast_to(shard[None], (devices, *shard.shape)), axis, 0, 0, tiled=True
    )


def collect(shard, axis, dim):
    return joined_along(copy_for_each(shard, axis), dim)


def gathered_once(shard, axis):
    leaves = jax.tree.leaves(shard)
    order = sorted(range(len(leaves)), key=lambda k: -leaves[k].size)
    width = (1, *leaves[order[0]].shape)[-1]
    lines = [
        jnp.pad(leaves[k].reshape(-1), (0, -leaves[k].size % width)).reshape(-1, width)
        for k in order
    ]
    both, at, found = (copy_for_each(jnp.concatenate(lines), axis), 0, {})
    for k, line in zip(order, lines):
        share = both[:, at : at + len(line)].reshape(len(both), -1)
        found[k] = share[:, : leaves[k].size].reshape(-1, *leaves[k].shape)
        at += len(line)
    numbers = iter(range(len(leaves)))
    return jax.tree.map(lambda _: found[next(numbers)], shard)


def combined_pairwise(pieces, combine):
    while len(jax.tree.leaves(pieces)[0]) > 1:
        pieces = jax.vmap(combine)(
            *(jax.tree.map(lambda part: part[side::2], pieces) for side in (0, 1))
        )
    return jax.tree.map(lambda part: part[0], pieces)


def combined_all(shard, axis, combine):
    pieces = gathered_once(shard, axis)
    return combined_pairwise(pieces, combine)


def rms_scale(values, gain):
    mean_square = jnp.mean(values * values, axis=-1, keepdims=True)
    return values * lax.rsqrt(mean_square + 1e-05) * gain


def rotate(values, places):
    half = values.shape[-1] // 2
    freq = 10000.0 ** (-(jnp.arange(half, dtype=jnp.float32) * 2.0 / values.shape[-1]))
    angle = places[..., None, None] * freq
    first = values[..., :half]
    second = values[..., half:]
    cosine = jnp.cos(angle)
    sine = jnp.sin(angle)
    return jnp.concatenate(
        [first * cosine - second * sine, second * cosine + first * sine], axis=-1
    )


def join_softmax(left, right):
    top = jnp.maximum(left[0], right[0])
    left_factor = jnp.exp(left[0] - top)
    right_factor = jnp.exp(right[0] - top)
    total = left[1] * left_factor + right[1] * right_factor
    acc = left[2] * left_factor[..., None] + right[2] * right_factor[..., None]
    return (top, total, acc)


def join_totals(left, right):
    top = jnp.maximum(left[0], right[0])
    return (top, left[1] * jnp.exp(left[0] - top) + right[1] * jnp.exp(right[0] - top))


def on_device(
    actions,
    lengths,
    embed,
    attn_gain,
    w_query,
    w_key,
    w_value,
    w_out,
    key_cache,
    value_cache,
    final_gain,
    head,
):
    seq_index = lax.axis_index(SEQ)
    seq_count = lax.axis_size(SEQ)
    robots, steps = actions.shape
    prompt_dev = key_cache.shape[1]
    width = key_cache.shape[2]
    col_block = w_query.shape[1]
    head_dim = HEAD_DIM
    heads = width // head_dim
    local_heads = col_block // head_dim
    scale = head_dim ** (-0.5)
    bins = jnp.arange(embed.shape[0], dtype=jnp.int32)
    onehot = (actions[:, :, None] == bins[None, None, :]).astype(jnp.bfloat16)
    inputs = jnp.einsum("rtb,bd->rtd", onehot, embed, preferred_element_type=jnp.float32)
    normed = rms_scale(inputs, attn_gain).astype(jnp.bfloat16)
    places = (lengths[:, None] + jnp.arange(steps, dtype=jnp.int32)[None, :]).astype(jnp.float32)
    prompt_places = seq_index * prompt_dev + jnp.arange(prompt_dev, dtype=jnp.int32)
    prompt_valid = prompt_places[None, :] < lengths[:, None]
    cache_keys = key_cache.reshape(robots, prompt_dev, heads, head_dim)
    cache_values = value_cache.reshape(robots, prompt_dev, heads, head_dim)
    empty = jnp.zeros((robots, 0, heads, head_dim), jnp.bfloat16)
    window_keys = empty
    window_values = empty
    rows = robots * steps
    block_norm = normed.reshape(rows, width)
    spread_rows = lax.all_to_all(block_norm, "grp", split_axis=1, concat_axis=0, tiled=True)
    terms = jnp.concatenate(
        [
            jnp.dot(spread_rows, w_query, preferred_element_type=jnp.float32),
            jnp.dot(spread_rows, w_key, preferred_element_type=jnp.float32),
            jnp.dot(spread_rows, w_value, preferred_element_type=jnp.float32),
        ],
        axis=1,
    )
    sums = sum_at_owner(terms, "grp", 0)

    def heads_of(flat):
        return flat.reshape(robots, steps, local_heads, head_dim)

    query = (
        rotate(heads_of(sums[:, :col_block]), places).astype(jnp.bfloat16).reshape(rows, col_block)
    )
    key = (
        rotate(heads_of(sums[:, col_block : 2 * col_block]), places)
        .astype(jnp.bfloat16)
        .reshape(rows, col_block)
    )
    value = sums[:, 2 * col_block :].astype(jnp.bfloat16)
    query, key, value = sent_together((query, key, value), SEQ, 1, 0)
    query = query.reshape(robots, steps, heads, head_dim)
    window_keys = jnp.concatenate(
        [window_keys, key.reshape(robots, steps, heads, head_dim)], axis=1
    )
    window_values = jnp.concatenate(
        [window_values, value.reshape(robots, steps, heads, head_dim)], axis=1
    )
    seen = 0 + steps
    window_index = jnp.arange(seen, dtype=jnp.int32)
    step_index = 0 + jnp.arange(steps, dtype=jnp.int32)
    window_valid = (window_index[None, :] <= step_index[:, None]) & (
        window_index % seq_count == seq_index
    )[None, :]
    prompt_mask = prompt_valid[:, None, None, :]
    window_mask = window_valid[None, :, None, :]
    prompt_scores = (
        jnp.einsum("rthd,rphd->rthp", query, cache_keys, preferred_element_type=jnp.float32) * scale
    )
    window_scores = (
        jnp.einsum("rthd,rjhd->rthj", query, window_keys, preferred_element_type=jnp.float32)
        * scale
    )
    prompt_scores = jnp.where(prompt_mask, prompt_scores, -1e30)
    window_scores = jnp.where(window_mask, window_scores, -1e30)
    local_max = jnp.maximum(jnp.max(prompt_scores, axis=-1), jnp.max(window_scores, axis=-1))
    prompt_e = jnp.where(prompt_mask, jnp.exp(prompt_scores - local_max[..., None]), 0.0)
    window_e = jnp.where(window_mask, jnp.exp(window_scores - local_max[..., None]), 0.0)
    total = jnp.sum(prompt_e, axis=-1) + jnp.sum(window_e, axis=-1)
    acc = jnp.einsum(
        "rthp,rphd->rthd",
        prompt_e.astype(jnp.bfloat16),
        cache_values,
        preferred_element_type=jnp.float32,
    )
    acc = acc + jnp.einsum(
        "rthj,rjhd->rthd",
        window_e.astype(jnp.bfloat16),
        window_values,
        preferred_element_type=jnp.float32,
    )
    total, acc = (total, acc)
    top, total, acc = merged_by_axis((local_max, total, acc), SEQ, join_softmax)
    attended = (acc / total[..., None]).astype(jnp.bfloat16).reshape(rows, width)
    spread_attended = lax.all_to_all(attended, "grp", split_axis=1, concat_axis=0, tiled=True)
    out_terms = jnp.dot(spread_attended, w_out, preferred_element_type=jnp.float32)
    out_part = sum_at_owner_2(out_terms.astype(jnp.bfloat16), "grp", 0)
    branch = collect(out_part, SEQ, 1)
    residual = inputs.reshape(rows, width) + branch
    final = rms_scale(residual, final_gain).astype(jnp.bfloat16)
    logits = lax.dot_general(
        final, head, (((1,), (1,)), ((), ())), preferred_element_type=jnp.float32
    )
    row_max = jnp.max(logits, axis=-1)
    local_total = jnp.sum(jnp.exp(logits - row_max[:, None]), axis=-1)
    top_logit, exp_total = combined_all((row_max, local_total), SEQ, join_totals)
    logprob = logits - top_logit[:, None] - jnp.log(exp_total)[:, None]
    result = logprob.reshape(robots, steps, logits.shape[1])
    return result


def solution(mesh):
    torus = Mesh(mesh.devices.reshape(4, 4, mesh.shape["grp"]), ("seq_0", "seq_1", "grp"))
    in_specs = (
        P("grp", None),
        P("grp"),
        P(),
        P(),
        P("grp", SEQ),
        P("grp", SEQ),
        P("grp", SEQ),
        P("grp", SEQ),
        P("grp", SEQ, None),
        P("grp", SEQ, None),
        P(),
        P(SEQ, None),
    )
    out_specs = P("grp", None, SEQ)
    return jax.shard_map(
        on_device, mesh=torus, in_specs=in_specs, out_specs=out_specs, check_vma=False
    )
```

profile of v0, /device:TPU:1, one launch (start us, length us, event | category | flops | bytes accessed | tf_op | source)
XLA Modules:
  0.0 184.5 jit_solution(1616942880006318692)
XLA Ops:
  0.0 1.6 copy-done
  1.6 1.2 multiply_reduce_fusion.1
  2.8 0.8 multiply_convert_fusion.1
  3.6 0.2 all_to_all.38
  3.8 18.6 %all_to_all.55 = bf16[14,16,256]{2,0,1:T(8,128)(2,1)S(1)} all-to-all(bf16[14,16,256]{2,0,1:T(8,128)(2,1)S(1)} %copy.58), channel_id=1, replica_groups=mesh['seq_0'=4,'seq_1'=4,'grp'=16] {'grp'}, dimensions={1} | all-to-all | bytes 229376 | tf_op jit(solution)/shard_map/all_to_all | solution.py:178
  22.5 1.1 fusion.65
  23.6 0.2 fusion.66
  23.8 0.2 fusion.67
  24.1 1.0 reshape.569
  25.0 4.2 %all-to-all-start.1 = ((f32[16,14,768]{2,1,0:T(8,128)}), f32[16,14,768]{2,1,0:T(8,128)}, u32[]{:S(2)}, u32[]{:S(2)}) async-start(f32[16,14,768]{2,1,0:T(8,128)} %reshape.569), calls=%async_computation.1 | async-start | bytes 1572864 | tf_op jit(solution)/shard_map/all_to_all | solution.py:18
  29.4 0.1 multiply_cosine_fusion
  29.6 22.2 %all-to-all-done.1 = f32[16,14,768]{2,1,0:T(8,128)} async-done(((f32[16,14,768]{2,1,0:T(8,128)}), f32[16,14,768]{2,1,0:T(8,128)}, u32[]{:S(2)}, u32[]{:S(2)}) %all-to-all-start.1) | async-done | bytes 688160 | tf_op jit(solution)/shard_map/all_to_all | solution.py:18
  51.8 1.2 reduce_sum.64
  53.1 0.1 subtract_convert_fusion.1
  53.2 0.1 pad_maximum_fusion.4
  53.3 0.1 pad_maximum_fusion.5
  53.4 19.9 %all_gather.15 = bf16[42,4096]{1,0:T(8,128)(2,1)S(1)} all-gather(bf16[42,256]{1,0:T(8,128)(2,1)S(1)} %pad_maximum_fusion.3), channel_id=1, replica_groups=mesh['seq_0'=4,'seq_1'=4,'grp'=16] {'seq_0','seq_1'}, dimensions={1}, use_global_device_ids=true | all-gather | bytes 365568 | tf_op jit(solution)/shard_map/all_gather | solution.py:25
  73.5 0.2 convolution_multiply_fusion
  73.7 0.2 copy.93
  73.8 0.1 fusion.45
  74.0 0.1 copy.78
  74.1 3.5 %fusion.63 = (f32[2,7,32]{1,2,0:T(8,128)S(1)}, f32[2,7,32,256]{3,1,2,0:T(8,128)S(1)}) fusion(bf16[2,7,32,128]{3,2,1,0:T(8,128)(2,1)S(1)} %bitcast.185, pred[2,256]{1,0:T(4,128)(4,1)S(1)} %broadcast_compare_fusion, bf16[2,256,4096]{2,1,0:T(8,128)(2,1)} %param.20), kind=kOutput, calls=%fused_computation.130 | convolution fusion | flops 29703744 | bytes 4770048 | tf_op jit(solution)/shard_map/rthd,rphd->rthp/dot_general | solution.py:218
  77.6 0.1 copy.66
  77.7 0.1 copy.70
  77.7 0.2 fusion.53
  77.9 0.2 copy.68
  78.1 0.3 fusion.23
  78.4 0.2 convolution_bitcast_fusion
  78.6 2.9 %fusion.20 = f32[2,7,32,128]{3,1,2,0:T(8,128)S(1)} fusion(f32[2,7,32,128]{3,1,2,0:T(8,128)S(1)} %convolution_bitcast_fusion, f32[2,7,32,256]{3,1,2,0:T(8,128)S(1)} %get-tuple-element.74, f32[2,7,32]{1,2,0:T(8,128)S(1)} %max.134, pred[2,256]{1,0:T(4,128)(4,1)S(1)} %broadcast_compare_fusion, bf16[2,256,4096]{2,1,0:T(8,128)(2,1)} %param.21), kind=kOutput, calls=%fused_computation.12 | convolution fusion | flops 29761536 | bytes 5114112 | tf_op jit(solution)/shard_map/rthp,rphd->rthd/dot_general | solution.py:230
  81.6 0.1 copy.79
  81.7 0.1 copy.72
  81.8 0.1 add.171
  82.0 10.7 %all-gather = f32[1824,128]{1,0:T(8,128)S(1)} all-gather(f32[456,128]{1,0:T(8,128)S(1)} %pad_maximum_fusion.1), channel_id=2, replica_groups=mesh['seq_0'=4,'seq_1'=4,'grp'=16] {'seq_0'}, dimensions={0}, use_global_device_ids=true | all-gather | bytes 1167360 | tf_op jit(solution)/shard_map/all_gather | solution.py:37
  92.8 0.4 fusion.30
  93.2 11.3 %all-gather.1 = f32[1824,128]{1,0:T(8,128)S(1)} all-gather(f32[456,128]{1,0:T(8,128)S(1)} %pad_maximum_fusion.2), channel_id=3, replica_groups=mesh['seq_0'=4,'seq_1'=4,'grp'=16] {'seq_1'}, dimensions={0}, use_global_device_ids=true | all-gather | bytes 1167360 | tf_op jit(solution)/shard_map/all_gather | solution.py:37
  105.7 0.8 div.27
  106.5 1.0 div.28
  107.5 0.8 mul.403
  108.3 1.7 mul.404
  110.0 0.8 mul.406
  110.8 1.7 mul.407
  112.5 0.8 mul.409
  113.3 1.7 mul.410
  115.0 0.8 mul.412
  115.8 1.7 mul.413
  117.5 0.8 mul.415
  118.3 1.7 mul.416
  120.0 0.8 mul.418
  120.8 1.7 mul.419
  122.5 1.7 divide_convert_fusion
  124.3 21.9 %all_to_all.56 = bf16[14,16,256]{2,0,1:T(8,128)(2,1)S(1)} all-to-all(bf16[14,16,256]{2,0,1:T(8,128)(2,1)S(1)} %copy.73), channel_id=1, replica_groups=mesh['seq_0'=4,'seq_1'=4,'grp'=16] {'grp'}, dimensions={1} | all-to-all | bytes 229376 | tf_op jit(solution)/shard_map/all_to_all | solution.py:245
  146.2 1.1 convolution_convert_fusion
  147.3 11.6 %all_to_all.57 = bf16[16,14,256]{2,1,0:T(8,128)(2,1)S(1)} all-to-all(bf16[16,14,256]{2,1,0:T(8,128)(2,1)S(1)} %reshape.586), channel_id=1, replica_groups=mesh['seq_0'=4,'seq_1'=4,'grp'=16] {'grp'}, dimensions={0} | all-to-all | bytes 229376 | tf_op jit(solution)/shard_map/all_to_all | solution.py:57
  158.9 0.7 broadcast_in_dim.49
  159.6 4.9 %all-to-all-start.4 = ((f32[16,14,256]{2,1,0:T(8,128)}), f32[16,14,256]{2,1,0:T(8,128)S(1)}, u32[]{:S(2)}, u32[]{:S(2)}) async-start(f32[16,14,256]{2,1,0:T(8,128)} %broadcast_in_dim.49), calls=%async_computation.4 | async-start | bytes 524288 | tf_op jit(solution)/shard_map/all_to_all | solution.py:69
  164.5 8.5 %all-to-all-done.4 = f32[16,14,256]{2,1,0:T(8,128)S(1)} async-done(((f32[16,14,256]{2,1,0:T(8,128)}), f32[16,14,256]{2,1,0:T(8,128)S(1)}, u32[]{:S(2)}, u32[]{:S(2)}) %all-to-all-start.4) | async-done | bytes 229408 | tf_op jit(solution)/shard_map/all_to_all | solution.py:69
  173.0 0.1 copy.74
  173.3 0.1 multiply_reduce_fusion
  173.4 0.1 rsqrt.21
  173.5 0.2 copy.92
  173.7 0.4 fusion.64
  174.0 0.2 exponential_reduce_fusion
  174.3 9.2 %all_to_all.58 = f32[16,2,14]{2,1,0:T(2,128)S(1)} all-to-all(f32[16,2,14]{2,1,0:T(2,128)S(1)} %broadcast_in_dim.50), channel_id=1, replica_groups=mesh['seq_0'=4,'seq_1'=4,'grp'=16] {'seq_0','seq_1'}, dimensions={0} | all-to-all | bytes 3584 | tf_op jit(solution)/shard_map/all_to_all | solution.py:69
  183.9 0.6 copy.77
  (101 shorter events, 2.5 us)
Async XLA Ops:
  0.0 1.6 copy-start
  0.0 23.6 %copy-start.1 = (bf16[256,256]{1,0:T(8,128)(2,1)S(1)}, bf16[256,256]{1,0:T(8,128)(2,1)}, u32[]{:S(2)}) copy-start(bf16[256,256]{1,0:T(8,128)(2,1)} %param.17) | copy-start | bytes 393220
  0.0 23.8 %copy-start.2 = (bf16[256,256]{1,0:T(8,128)(2,1)S(1)}, bf16[256,256]{1,0:T(8,128)(2,1)}, u32[]{:S(2)}) copy-start(bf16[256,256]{1,0:T(8,128)(2,1)} %param.18) | copy-start | bytes 393220
  2.8 26.5 %copy-start.5 = (s32[2]{0:T(128)S(1)}, s32[2]{0:T(128)}, u32[]{:S(2)}) copy-start(s32[2]{0:T(128)} %param.13) | copy-start | bytes 28
  25.0 26.8 %all-to-all-start.1 = ((f32[16,14,768]{2,1,0:T(8,128)}), f32[16,14,768]{2,1,0:T(8,128)}, u32[]{:S(2)}, u32[]{:S(2)}) async-start(f32[16,14,768]{2,1,0:T(8,128)} %reshape.569), calls=%async_computation.1 | async-start | bytes 1572864 | tf_op jit(solution)/shard_map/all_to_all | solution.py:18
  122.5 51.1 %copy-start.4 = (f32[4096]{0:T(1024)S(1)}, f32[4096]{0:T(1024)}, u32[]{:S(2)}) copy-start(f32[4096]{0:T(1024)} %param.22) | copy-start | bytes 49156
  124.2 49.5 %copy-start.3 = (bf16[16,4096]{1,0:T(8,128)(2,1)S(1)}, bf16[16,4096]{1,0:T(8,128)(2,1)}, u32[]{:S(2)}) copy-start(bf16[16,4096]{1,0:T(8,128)(2,1)} %param.23) | copy-start | bytes 393220
  159.6 13.4 %all-to-all-start.4 = ((f32[16,14,256]{2,1,0:T(8,128)}), f32[16,14,256]{2,1,0:T(8,128)S(1)}, u32[]{:S(2)}, u32[]{:S(2)}) async-start(f32[16,14,256]{2,1,0:T(8,128)} %broadcast_in_dim.49), calls=%async_computation.4 | async-start | bytes 524288 | tf_op jit(solution)/shard_map/all_to_all | solution.py:69
where the time goes:
time: 185 us
  blocking collectives  103 us (56%)
  waiting for transfers between devices  30.7 us (17%)
  local copies, waits for them, and re-layouts  24.2 us (13%)
  matrix products  10.8 us (6%)
  starting transfers between devices  9.04 us (5%)
  other arithmetic  5.88 us (3%)
    all_to_all x1, waiting for transfers between devices, sum_at_owner(): lax.all_to_all(pieces, axis, split_axis=0, concat_axis=0, tiled=True)  22.2 us
    all_gather x2, blocking collectives, all_in_one(): both, at, found = (lax.all_gather(jnp.concatenate(lines), axis), 0, {})  22.1 us
    all_to_all x1, blocking collectives, on_device(): lax.all_to_all(attended, 'grp', split_axis=1, concat_axis=0, tiled=True)  21.9 us
    all_gather x1, blocking collectives, sent_together(): out = lax.all_gather(both, axis, axis=dim, tiled=True)  19.9 us
    all_to_all x1, blocking collectives, on_device(): lax.all_to_all(block_norm, 'grp', split_axis=1, concat_axis=0, tiled=True)  18.6 us
    mul x12, local copies, waits for them, and re-layouts, join_softmax(): acc = left[2] * left_factor[..., None] + right[2] * right_factor[..., None]  15 us
    all_to_all x1, blocking collectives, sum_at_owner_2(): lax.all_to_all(split_up(shard, dim, devices), axis, 0, 0, tiled=True)  11.6 us
    all_to_all x1, blocking collectives, copy_for_each(): lax.all_to_all(jnp.broadcast_to(shard[None], (devices, *shard.shape)), ax...  9.25 us
  transfers between devices with their start and end apart: 2, of which 2 were waited for; matrix products, arithmetic and copies ran while one was open for 0% of the time, Pallas kernels for 0%

commit v1 on v0

--- a/solution.py
+++ b/solution.py
@@ -242,7 +242,10 @@
     total, acc = (total, acc)
     top, total, acc = merged_by_axis((local_max, total, acc), SEQ, join_softmax)
     attended = (acc / total[..., None]).astype(jnp.bfloat16).reshape(rows, width)
-    spread_attended = lax.all_to_all(attended, "grp", split_axis=1, concat_axis=0, tiled=True)
+    spread_attended = jnp.concatenate(
+        lax.all_to_all(jnp.stack(jnp.split(attended, lax.axis_size("grp"), axis=1)), "grp", 0, 0),
+        axis=0,
+    )
     out_terms = jnp.dot(spread_attended, w_out, preferred_element_type=jnp.float32)
     out_part = sum_at_owner_2(out_terms.astype(jnp.bfloat16), "grp", 0)
     branch = collect(out_part, SEQ, 1)

time: 185 us -> 171 us (0.924)
  local copies, waits for them, and re-layouts: 24.2 us -> 10.9 us
    mul x12 -> x6, local copies, waits for them, and re-layouts: 15 us -> 0.68 us  [join_softmax(): acc = left[2] * left_factor[..., None] + right[2] * right_factor[..., None]]
where the time goes in v1:
time: 171 us; the launch traced here: 170 us
  blocking collectives  103 us (60%)
  waiting for transfers between devices  30.7 us (18%)
  local copies, waits for them, and re-layouts  10.9 us (6%)
  matrix products  10.8 us (6%)
  starting transfers between devices  9.04 us (5%)
  other arithmetic  4.36 us (3%)
    all_to_all x1, waiting for transfers between devices, sum_at_owner(): lax.all_to_all(pieces, axis, split_axis=0, concat_axis=0, tiled=True)  22.2 us
    all_gather x2, blocking collectives, all_in_one(): both, at, found = (lax.all_gather(jnp.concatenate(lines), axis), 0, {})  22.1 us
    all_to_all x1, blocking collectives, on_device(): lax.all_to_all(jnp.stack(jnp.split(attended, lax.axis_size('grp'), axis=1...  21.9 us
    all_gather x1, blocking collectives, sent_together(): out = lax.all_gather(both, axis, axis=dim, tiled=True)  19.9 us
    all_to_all x1, blocking collectives, on_device(): lax.all_to_all(block_norm, 'grp', split_axis=1, concat_axis=0, tiled=True)  18.6 us
    all_to_all x1, blocking collectives, sum_at_owner_2(): lax.all_to_all(split_up(shard, dim, devices), axis, 0, 0, tiled=True)  11.6 us
    all_to_all x1, blocking collectives, copy_for_each(): lax.all_to_all(jnp.broadcast_to(shard[None], (devices, *shard.shape)), ax...  9.25 us
    all_to_all x1, waiting for transfers between devices, copy_for_each(): lax.all_to_all(jnp.broadcast_to(shard[None], (devices, *shard.shape)), ax...  8.5 us
  transfers between devices with their start and end apart: 2, of which 2 were waited for; matrix products, arithmetic and copies ran while one was open for 0% of the time, Pallas kernels for 0%

profile of v1, /device:TPU:1, one launch (start us, length us, event | category | flops | bytes accessed | tf_op | source)
XLA Modules:
  0.0 170.0 jit_solution(11770587351404022809)
XLA Ops:
  0.0 1.6 copy-done
  1.6 1.2 multiply_reduce_fusion.1
  2.8 0.8 multiply_convert_fusion.1
  3.6 0.2 all_to_all.29
  3.8 18.6 %all_to_all.44 = bf16[14,16,256]{2,0,1:T(8,128)(2,1)S(1)} all-to-all(bf16[14,16,256]{2,0,1:T(8,128)(2,1)S(1)} %copy.44), channel_id=1, replica_groups=mesh['seq_0'=4,'seq_1'=4,'grp'=16] {'grp'}, dimensions={1} | all-to-all | bytes 229376 | tf_op jit(solution)/shard_map/all_to_all | solution.py:178
  22.5 1.1 fusion.65
  23.6 0.2 fusion.66
  23.8 0.2 fusion.67
  24.1 1.0 reshape.558
  25.0 4.2 %all-to-all-start.1 = ((f32[16,14,768]{2,1,0:T(8,128)}), f32[16,14,768]{2,1,0:T(8,128)}, u32[]{:S(2)}, u32[]{:S(2)}) async-start(f32[16,14,768]{2,1,0:T(8,128)} %reshape.558), calls=%async_computation.1 | async-start | bytes 1572864 | tf_op jit(solution)/shard_map/all_to_all | solution.py:18
  29.4 0.1 multiply_cosine_fusion
  29.6 22.2 %all-to-all-done.1 = f32[16,14,768]{2,1,0:T(8,128)} async-done(((f32[16,14,768]{2,1,0:T(8,128)}), f32[16,14,768]{2,1,0:T(8,128)}, u32[]{:S(2)}, u32[]{:S(2)}) %all-to-all-start.1) | async-done | bytes 688160 | tf_op jit(solution)/shard_map/all_to_all | solution.py:18
  51.8 1.2 reduce_sum.64
  53.1 0.1 subtract_convert_fusion.1
  53.2 0.1 pad_maximum_fusion.4
  53.3 0.1 pad_maximum_fusion.5
  53.4 19.9 %all_gather.15 = bf16[42,4096]{1,0:T(8,128)(2,1)S(1)} all-gather(bf16[42,256]{1,0:T(8,128)(2,1)S(1)} %pad_maximum_fusion.3), channel_id=1, replica_groups=mesh['seq_0'=4,'seq_1'=4,'grp'=16] {'seq_0','seq_1'}, dimensions={1}, use_global_device_ids=true | all-gather | bytes 365568 | tf_op jit(solution)/shard_map/all_gather | solution.py:25
  73.5 0.2 convolution_multiply_fusion
  73.7 0.2 copy.85
  73.8 0.1 fusion.45
  74.0 0.1 copy.63
  74.1 3.5 %fusion.63 = (f32[2,7,32]{1,2,0:T(8,128)S(1)}, f32[2,7,32,256]{3,1,2,0:T(8,128)S(1)}) fusion(bf16[2,7,32,128]{3,2,1,0:T(8,128)(2,1)S(1)} %bitcast.262, pred[2,256]{1,0:T(4,128)(4,1)S(1)} %broadcast_compare_fusion, bf16[2,256,4096]{2,1,0:T(8,128)(2,1)} %param.20), kind=kOutput, calls=%fused_computation.162 | convolution fusion | flops 29703744 | bytes 4770048 | tf_op jit(solution)/shard_map/rthd,rphd->rthp/dot_general | solution.py:218
  77.6 0.1 copy.52
  77.7 0.2 fusion.53
  77.9 0.2 copy.54
  78.1 0.3 fusion.23
  78.4 0.2 convolution_bitcast_fusion
  78.6 2.9 %fusion.20 = f32[2,7,32,128]{3,1,2,0:T(8,128)S(1)} fusion(f32[2,7,32,128]{3,1,2,0:T(8,128)S(1)} %convolution_bitcast_fusion, f32[2,7,32,256]{3,1,2,0:T(8,128)S(1)} %get-tuple-element.74, f32[2,7,32]{1,2,0:T(8,128)S(1)} %max.134, pred[2,256]{1,0:T(4,128)(4,1)S(1)} %broadcast_compare_fusion, bf16[2,256,4096]{2,1,0:T(8,128)(2,1)} %param.21), kind=kOutput, calls=%fused_computation.12 | convolution fusion | flops 29761536 | bytes 5114112 | tf_op jit(solution)/shard_map/rthp,rphd->rthd/dot_general | solution.py:230
  81.6 0.1 copy.64
  81.7 0.1 copy.58
  82.0 10.7 %all-gather = f32[1824,128]{1,0:T(8,128)S(1)} all-gather(f32[456,128]{1,0:T(8,128)S(1)} %pad_maximum_fusion.1), channel_id=2, replica_groups=mesh['seq_0'=4,'seq_1'=4,'grp'=16] {'seq_0'}, dimensions={0}, use_global_device_ids=true | all-gather | bytes 1167360 | tf_op jit(solution)/shard_map/all_gather | solution.py:37
  92.8 0.4 fusion.30
  93.2 11.3 %all-gather.1 = f32[1824,128]{1,0:T(8,128)S(1)} all-gather(f32[456,128]{1,0:T(8,128)S(1)} %pad_maximum_fusion.2), channel_id=3, replica_groups=mesh['seq_0'=4,'seq_1'=4,'grp'=16] {'seq_1'}, dimensions={0}, use_global_device_ids=true | all-gather | bytes 1167360 | tf_op jit(solution)/shard_map/all_gather | solution.py:37
  104.6 0.7 fusion.57
  105.4 1.0 squeeze.92
  107.1 0.1 mul.412
  107.3 0.2 copy.81
  107.5 0.1 div.26
  107.6 0.2 copy.83
  107.8 0.1 mul.397
  107.9 0.2 copy.76
  108.1 0.1 mul.400
  108.2 0.2 copy.77
  108.4 0.1 mul.403
  108.6 0.2 copy.78
  108.7 0.1 mul.406
  108.9 0.2 copy.79
  109.0 0.1 mul.409
  109.2 0.2 copy.80
  109.4 0.1 divide_convert_fusion
  109.7 21.9 %all_to_all.45 = bf16[16,14,256]{2,1,0:T(8,128)(2,1)S(1)} all-to-all(bf16[16,14,256]{2,1,0:T(8,128)(2,1)S(1)} %constant_dynamic-update-slice_fusion), channel_id=1, replica_groups=mesh['seq_0'=4,'seq_1'=4,'grp'=16] {'grp'}, dimensions={0} | all-to-all | bytes 229376 | tf_op jit(solution)/shard_map/all_to_all | solution.py:246
  131.6 0.2 convolution_convert_fusion
  131.9 11.6 %all_to_all.46 = bf16[16,14,256]{2,1,0:T(8,128)(2,1)S(1)} all-to-all(bf16[16,14,256]{2,1,0:T(8,128)(2,1)S(1)} %reshape.576), channel_id=1, replica_groups=mesh['seq_0'=4,'seq_1'=4,'grp'=16] {'grp'}, dimensions={0} | all-to-all | bytes 229376 | tf_op jit(solution)/shard_map/all_to_all | solution.py:57
  143.4 0.7 broadcast_in_dim.49
  144.2 4.9 %all-to-all-start.4 = ((f32[16,14,256]{2,1,0:T(8,128)}), f32[16,14,256]{2,1,0:T(8,128)S(1)}, u32[]{:S(2)}, u32[]{:S(2)}) async-start(f32[16,14,256]{2,1,0:T(8,128)} %broadcast_in_dim.49), calls=%async_computation.4 | async-start | bytes 524288 | tf_op jit(solution)/shard_map/all_to_all | solution.py:69
  149.1 8.5 %all-to-all-done.4 = f32[16,14,256]{2,1,0:T(8,128)S(1)} async-done(((f32[16,14,256]{2,1,0:T(8,128)}), f32[16,14,256]{2,1,0:T(8,128)S(1)}, u32[]{:S(2)}, u32[]{:S(2)}) %all-to-all-start.4) | async-done | bytes 229408 | tf_op jit(solution)/shard_map/all_to_all | solution.py:69
  157.6 0.1 copy.59
  157.8 0.1 multiply_reduce_fusion
  158.0 0.1 rsqrt.21
  158.0 0.2 copy.84
  158.2 1.3 fusion.64
  159.5 0.2 exponential_reduce_fusion
  159.7 9.3 %all_to_all.47 = f32[16,2,14]{2,1,0:T(2,128)S(1)} all-to-all(f32[16,2,14]{2,1,0:T(2,128)S(1)} %broadcast_in_dim.50), channel_id=1, replica_groups=mesh['seq_0'=4,'seq_1'=4,'grp'=16] {'seq_0','seq_1'}, dimensions={0} | all-to-all | bytes 3584 | tf_op jit(solution)/shard_map/all_to_all | solution.py:69
  169.4 0.6 copy.62
  (123 shorter events, 2.6 us)
Async XLA Ops:
  0.0 1.6 copy-start
  0.0 23.6 %copy-start.1 = (bf16[256,256]{1,0:T(8,128)(2,1)S(1)}, bf16[256,256]{1,0:T(8,128)(2,1)}, u32[]{:S(2)}) copy-start(bf16[256,256]{1,0:T(8,128)(2,1)} %param.17) | copy-start | bytes 393220
  0.0 23.8 %copy-start.2 = (bf16[256,256]{1,0:T(8,128)(2,1)S(1)}, bf16[256,256]{1,0:T(8,128)(2,1)}, u32[]{:S(2)}) copy-start(bf16[256,256]{1,0:T(8,128)(2,1)} %param.18) | copy-start | bytes 393220
  2.8 26.5 %copy-start.5 = (s32[2]{0:T(128)S(1)}, s32[2]{0:T(128)}, u32[]{:S(2)}) copy-start(s32[2]{0:T(128)} %param.13) | copy-start | bytes 28
  25.0 26.8 %all-to-all-start.1 = ((f32[16,14,768]{2,1,0:T(8,128)}), f32[16,14,768]{2,1,0:T(8,128)}, u32[]{:S(2)}, u32[]{:S(2)}) async-start(f32[16,14,768]{2,1,0:T(8,128)} %reshape.558), calls=%async_computation.1 | async-start | bytes 1572864 | tf_op jit(solution)/shard_map/all_to_all | solution.py:18
  108.2 23.4 %copy-start.3 = (bf16[256,256]{1,0:T(8,128)(2,1)S(1)}, bf16[256,256]{1,0:T(8,128)(2,1)}, u32[]{:S(2)}) copy-start(bf16[256,256]{1,0:T(8,128)(2,1)} %param.19) | copy-start | bytes 393220
  109.3 48.9 %copy-start.4 = (f32[4096]{0:T(1024)S(1)}, f32[4096]{0:T(1024)}, u32[]{:S(2)}) copy-start(f32[4096]{0:T(1024)} %param.22) | copy-start | bytes 49156
  144.2 13.4 %all-to-all-start.4 = ((f32[16,14,256]{2,1,0:T(8,128)}), f32[16,14,256]{2,1,0:T(8,128)S(1)}, u32[]{:S(2)}, u32[]{:S(2)}) async-start(f32[16,14,256]{2,1,0:T(8,128)} %broadcast_in_dim.49), calls=%async_computation.4 | async-start | bytes 524288 | tf_op jit(solution)/shard_map/all_to_all | solution.py:69
